TPU v7x, 32 devices: a whole 2x2x4 slice. The times are simulated.
32 devices in a mesh: dp: 2 (over x), ep: 16 (over y, z, core).
Axes of the slice: x: 2, y: 2, z: 4, core: 2. Of those that a mesh axis runs over, the one named last changes fastest.
Arguments:
- x: bfloat16 [2, 16, 512, 1280], P('dp', 'ep'), parts along dimension 0
- expert: int32 [2, 16, 512, 1], P('dp', 'ep'), parts along dimension 0
- slot: int32 [2, 16, 512, 1], P('dp', 'ep'), parts along dimension 0
- gate: float32 [2, 16, 512, 1], P('dp', 'ep'), parts along dimension 0
- w_gate: bfloat16 [32, 1280, 8192], P('ep')
- w_up: bfloat16 [32, 1280, 8192], P('ep')
- w_down: bfloat16 [32, 8192, 1280], P('ep')
- s_gate: bfloat16 [1280, 8192], replicated
- s_up: bfloat16 [1280, 8192], replicated
- s_down: bfloat16 [8192, 1280], replicated
Outputs:
- y: bfloat16 [2, 16, 512, 1280], P('dp', 'ep'), parts along dimension 0
There are 2 independent parts. A program takes and returns all parts, laid end to end along the dimension named above; an argument that names none is the same for every part.
All inputs are finite; a program needn't handle non-finite values.
Results may differ from a plain program's by a relative error of at most 0.009.
Values are sent between devices in bfloat16 or wider.
A program may use at most 2 GiB of HBM per device.

v0:
```python
import jax
import jax.numpy as jnp
from jax import lax
from jax.sharding import NamedSharding, PartitionSpec as P


def einsum(form, a, b):
    return jnp.einsum(form, a.astype(jnp.float32), b.astype(jnp.float32))


def for_all(x, s_gate, s_up, s_down):
    h = jax.nn.silu(einsum("...d,df->...f", x, s_gate)) * einsum("...d,df->...f", x, s_up)
    return einsum("...f,fd->...d", h.astype(jnp.bfloat16), s_down)


def solution(mesh):
    def placed(v, *spec):
        return lax.with_sharding_constraint(v, NamedSharding(mesh, P(*spec)))

    def step(x, expert, slot, gate, w_gate, w_up, w_down, s_gate, s_up, s_down):
        experts, (tokens, top) = w_gate.shape[0], expert.shape[2:]
        slots = 5 * tokens * top // (4 * experts)
        to_expert = jax.nn.one_hot(expert, experts, dtype=jnp.bfloat16)
        to_slot = jax.nn.one_hot(slot, slots, dtype=jnp.bfloat16)
        weighted = to_expert * gate[..., None].astype(jnp.bfloat16)
        dispatch = einsum("abtke,abtkc->abtec", to_expert, to_slot).astype(jnp.bfloat16)
        combine = einsum("abtke,abtkc->abtec", weighted, to_slot).astype(jnp.bfloat16)
        z = einsum("abtec,abtd->aebcd", dispatch, x).astype(jnp.bfloat16)
        z = placed(z, "dp", None, "ep", None, None)
        z = placed(z, "dp", "ep", None, None, None)
        h = jax.nn.silu(einsum("aebcd,edf->aebcf", z, w_gate))
        h = (h * einsum("aebcd,edf->aebcf", z, w_up)).astype(jnp.bfloat16)
        out = einsum("aebcf,efd->aebcd", h, w_down).astype(jnp.bfloat16)
        out = placed(out, "dp", "ep", None, None, None)
        out = placed(out, "dp", None, "ep", None, None)
        y = einsum("abtec,aebcd->abtd", combine, out)
        return (y + for_all(x, s_gate, s_up, s_down)).astype(jnp.bfloat16)

    return step
```

profile of v0, /device:TPU:14, one launch (start us, length us, event | category | flops | bytes accessed | tf_op | source)
XLA Modules:
  0.0 225.0 jit_solution(15181032383264070492)
XLA Ops:
  0.0 0.0 copy-start
  0.0 0.8 convert_bitcast_fusion
  0.8 0.7 convert_bitcast_fusion.1
  1.5 0.0 copy-start.1
  1.5 0.6 copy-done.1
  2.1 0.0 copy-done
  2.1 2.2 convolution_convert_fusion
  4.3 3.6 %reshape.27 = bf16[1,16,2,1,20,1280]{5,2,1,4,3,0:T(2,128)(2,1)S(1)} reshape(bf16[32,20,1280]{2,0,1:T(8,128)(2,1)} %convolution_convert_fusion) | data formatting | bytes 3276800 | tf_op jit(solution)/sharding_constraint;jit(solution)/sharding_constraint | solution.py:18
  8.0 1.1 copy.3
  9.1 43.8 %all-to-all.4 = bf16[1,16,2,1,20,1280]{5,2,4,3,0,1:T(2,128)(2,1)S(1)} all-to-all(bf16[1,16,2,1,20,1280]{5,2,4,3,0,1:T(2,128)(2,1)S(1)} %copy.3), channel_id=1, replica_groups=mesh['dp'=2,'ep'=16] {'ep'}, dimensions={1} | all-to-all | bytes 3276800 | tf_op jit(solution)/sharding_constraint;jit(solution)/sharding_constraint | solution.py:18
  52.9 30.1 %fusion.2 = f32[2,16,20,8192]{3,2,1,0:T(8,128)} fusion(bf16[2,1280,8192]{2,1,0:T(8,128)(2,1)} %param.5, bf16[1,16,2,1,20,1280]{5,2,4,3,0,1:T(2,128)(2,1)S(1)} %all-to-all.4), kind=kOutput, calls=%fused_computation.2 | convolution fusion | flops 13421772800 | bytes 64552960 | tf_op jit(solution)/aebcd,edf->aebcf/dot_general | solution.py:8
  83.1 30.2 %fusion.83 = bf16[2,16,20,8192]{3,2,1,0:T(8,128)(2,1)} fusion(f32[2,16,20,8192]{3,2,1,0:T(8,128)} %fusion.2, bf16[2,1280,8192]{2,1,0:T(8,128)(2,1)} %param.4, bf16[1,16,2,1,20,1280]{5,2,4,3,0,1:T(2,128)(2,1)S(1)} %all-to-all.4), kind=kOutput, calls=%fused_computation.20.clone.clone.clone.clone.clone.1 | convolution fusion | flops 13453230080 | bytes 75038720 | tf_op jit(solution)/aebcd,edf->aebcf/dot_general | solution.py:8
  113.2 0.0 copy-start.4
  113.2 0.0 copy-start.3
  113.2 24.2 %fusion.31 = bf16[1,2,16,1,20,1280]{5,4,2,1,3,0:T(8,128)(2,1)S(1)} fusion(bf16[2,8192,1280]{2,1,0:T(8,128)(2,1)} %param.6, bf16[2,16,20,8192]{3,2,1,0:T(8,128)(2,1)} %fusion.83), kind=kOutput, calls=%fused_computation.28 | convolution fusion | flops 13422592000 | bytes 54067200 | tf_op jit(solution)/aebcf,efd->aebcd/dot_general | solution.py:8
  137.5 2.9 %copy.5 = bf16[1,2,16,1,20,1280]{5,1,4,3,0,2:T(2,128)(2,1)} copy(bf16[1,2,16,1,20,1280]{5,4,2,1,3,0:T(8,128)(2,1)S(1)} %fusion.31) | data formatting | bytes 3276800 | tf_op jit(solution)/sharding_constraint;jit(solution)/sharding_constraint | solution.py:18
  140.3 6.0 %all-to-all-start.1 = ((bf16[1,2,16,1,20,1280]{5,1,4,3,0,2:T(2,128)(2,1)}), bf16[1,2,16,1,20,1280]{5,1,4,3,0,2:T(2,128)(2,1)S(1)}, u32[]{:S(2)}, u32[]{:S(2)}) async-start(bf16[1,2,16,1,20,1280]{5,1,4,3,0,2:T(2,128)(2,1)} %copy.5), calls=%async_computation.1 | async-start | bytes 3276800 | tf_op jit(solution)/sharding_constraint;jit(solution)/sharding_constraint | solution.py:18
  146.4 0.0 copy-done.4
  146.4 0.0 copy-done.3
  146.4 0.0 copy-start.2
  146.4 18.4 %fusion.46 = f32[512,8192]{1,0:T(8,128)} fusion(bf16[1280,8192]{1,0:T(8,128)(2,1)} %param.7, bf16[1,1,512,1280]{3,2,1,0:T(8,128)(2,1)S(1)} %copy-done), kind=kOutput, calls=%fused_computation.35 | convolution fusion | flops 10737418240 | bytes 39059456 | tf_op jit(solution)/...d,df->...f/dot_general | solution.py:8
  164.9 19.3 %all-to-all-done.1 = bf16[1,2,16,1,20,1280]{5,1,4,3,0,2:T(2,128)(2,1)S(1)} async-done(((bf16[1,2,16,1,20,1280]{5,1,4,3,0,2:T(2,128)(2,1)}), bf16[1,2,16,1,20,1280]{5,1,4,3,0,2:T(2,128)(2,1)S(1)}, u32[]{:S(2)}, u32[]{:S(2)}) %all-to-all-start.1) | async-done | bytes 1638432 | tf_op jit(solution)/sharding_constraint;jit(solution)/sharding_constraint | solution.py:18
  184.1 2.8 %copy.6 = bf16[1,16,2,1,20,1280]{5,2,1,4,3,0:T(2,128)(2,1)} copy(bf16[1,16,2,1,20,1280]{5,2,4,3,0,1:T(2,128)(2,1)S(1)} %bitcast.180) | data formatting | bytes 3276800 | tf_op jit(solution)/sharding_constraint;jit(solution)/sharding_constraint | solution.py:18
  186.9 3.8 %reshape.64 = bf16[32,20,1280]{2,0,1:T(8,128)(2,1)S(1)} reshape(bf16[1,16,2,1,20,1280]{5,2,1,4,3,0:T(2,128)(2,1)} %copy.6) | data formatting | bytes 3276800
  190.7 0.0 copy-done.2
  190.8 2.7 %convolution_bitcast_fusion = f32[512,1280]{1,0:T(8,128)} fusion(bf16[32,20,1280]{2,0,1:T(8,128)(2,1)S(1)} %reshape.64, f32[512,20]{0,1:T(8,128)S(1)} %copy-done.2, f32[512,32]{0,1:T(8,128)S(1)} %fusion.59), kind=kOutput, calls=%fused_computation.25 | convolution fusion | flops 839516160 | bytes 4366336 | tf_op jit(solution)/abtec,aebcd->abtd/dot_general | solution.py:8
  193.5 31.6 %fusion.38 = bf16[1,1,512,1280]{3,2,1,0:T(8,128)(2,1)} fusion(f32[512,1280]{1,0:T(8,128)} %convolution_bitcast_fusion, bf16[8192,1280]{1,0:T(8,128)(2,1)} %param.9, bf16[1280,8192]{1,0:T(8,128)(2,1)} %param.8, f32[512,8192]{1,0:T(8,128)} %fusion.46, bf16[1,1,512,1280]{3,2,1,0:T(8,128)(2,1)S(1)} %copy-done), kind=kOutput, calls=%fused_computation.29 | convolution fusion | flops 21501313024 | bytes 63963136 | tf_op jit(solution)/...f,fd->...d/dot_general | solution.py:8
  (2 shorter events, 0.0 us)
Async XLA Ops:
  0.0 2.1 copy-start
  1.5 0.6 copy-start.1
  113.2 33.2 %copy-start.4 = (f32[1,1,512,1]{2,3,1,0:T(1,128)S(1)}, f32[1,1,512,1]{2,3,1,0:T(1,128)}, u32[]{:S(2)}) copy-start(f32[1,1,512,1]{2,3,1,0:T(1,128)} %param.1) | copy-start | bytes 6148
  113.2 33.2 %copy-start.3 = (s32[1,1,512,1]{2,3,1,0:T(1,128)S(1)}, s32[1,1,512,1]{2,3,1,0:T(1,128)}, u32[]{:S(2)}) copy-start(s32[1,1,512,1]{2,3,1,0:T(1,128)} %param) | copy-start | bytes 6148
  140.3 43.8 %all-to-all-start.1 = ((bf16[1,2,16,1,20,1280]{5,1,4,3,0,2:T(2,128)(2,1)}), bf16[1,2,16,1,20,1280]{5,1,4,3,0,2:T(2,128)(2,1)S(1)}, u32[]{:S(2)}, u32[]{:S(2)}) async-start(bf16[1,2,16,1,20,1280]{5,1,4,3,0,2:T(2,128)(2,1)} %copy.5), calls=%async_computation.1 | async-start | bytes 3276800 | tf_op jit(solution)/sharding_constraint;jit(solution)/sharding_constraint | solution.py:18
  146.4 44.3 %copy-start.2 = (f32[512,20]{0,1:T(8,128)S(1)}, f32[512,20]{0,1:T(8,128)}, u32[]{:S(2)}) copy-start(f32[512,20]{0,1:T(8,128)} %copy-done.1) | copy-start | bytes 122884
where the time goes:
time: 226 us; the launch traced here: 225 us
  matrix products  139 us (62%)
  blocking collectives  43.8 us (19%)
  waiting for transfers between devices  19.3 us (9%)
  local copies, waits for them, and re-layouts  14.9 us (7%)
  starting transfers between devices  6.03 us (3%)
    dot_general x7, matrix products, einsum(): return jnp.einsum(form, a.astype(jnp.float32), b.astype(jnp.float32))  139 us
    another operation x1, blocking collectives, placed(): return lax.with_sharding_constraint(v, NamedSharding(mesh, P(*spec)))  43.8 us
    another operation x1, waiting for transfers between devices, placed(): return lax.with_sharding_constraint(v, NamedSharding(mesh, P(*spec)))  19.3 us
    another operation x4, local copies, waits for them, and re-layouts, placed(): return lax.with_sharding_constraint(v, NamedSharding(mesh, P(*spec)))  10.5 us
    another operation x1, starting transfers between devices, placed(): return lax.with_sharding_constraint(v, NamedSharding(mesh, P(*spec)))  6.03 us
  transfers between devices with their start and end apart: 1, of which 1 were waited for; matrix products, arithmetic and copies ran while one was open for 8% of the time, Pallas kernels for 0%

commit v1 on v0

v1 whole, which is shorter than its diff:
```python
import functools

import jax
import jax.numpy as jnp
from jax import lax
from jax.experimental import pallas as pl
from jax.experimental.pallas import tpu as pltpu
from jax.sharding import PartitionSpec as P

MESH = pl.DeviceIdType.MESH
N = 16
SLOTS, HEAD = 20, 16
TAIL = SLOTS - HEAD
ROWS = N * SLOTS
TILE = 512
RING = 5
FIRST = 8

BF16, F32, I32 = jnp.bfloat16, jnp.float32, jnp.int32
OFFSETS = [(y, z, c) for z in (2, 1, 3, 0) for y in (1, 0) for c in (1, 0) if (y, z, c) != (0, 0, 0)]


def dot(a, b):
    return jnp.dot(a, b, preferred_element_type=F32)


def rows_of(blocks, half):
    left, right = [], []
    for s in range(N):
        left.append(blocks[s, 0:HEAD])
        right.append(blocks[s, HEAD : 2 * HEAD])
    top = lax.broadcasted_iota(I32, (2 * TAIL, half), 0) < TAIL
    for p in range(N // 2):
        a = blocks[2 * p, 2 * HEAD :].astype(F32)
        b = blocks[2 * p + 1, 2 * HEAD :].astype(F32)
        left.append(jnp.where(top, a, pltpu.roll(b, TAIL, 0)).astype(BF16))
        right.append(jnp.where(top, pltpu.roll(a, TAIL, 0), b).astype(BF16))
    return left, right


def store_rows(blocks, rows, half):
    left, right = rows_of(blocks, half)
    at = 0
    for a, b in zip(left, right):
        n = a.shape[0]
        rows[at : at + n, 0:half] = a
        rows[at : at + n, half:] = b
        at += n


def store_blocks(total, blocks, half):
    for s in range(N):
        blocks[s, 0:HEAD] = total[HEAD * s : HEAD * (s + 1), 0:half].astype(BF16)
        blocks[s, HEAD : 2 * HEAD] = total[HEAD * s : HEAD * (s + 1), half:].astype(BF16)
    top = lax.broadcasted_iota(I32, (2 * TAIL, half), 0) < TAIL
    for p in range(N // 2):
        at = N * HEAD + 2 * TAIL * p
        a = total[at : at + 2 * TAIL, 0:half]
        b = total[at : at + 2 * TAIL, half:]
        blocks[2 * p, 2 * HEAD :] = jnp.where(top, a, pltpu.roll(b, TAIL, 0)).astype(BF16)
        blocks[2 * p + 1, 2 * HEAD :] = jnp.where(top, pltpu.roll(a, TAIL, 0), b).astype(BF16)


def kernel(
    x_hbm, expert_ref, slot_ref, gate_ref, wg, wu, wd, sg, su, sd, y_ref,
    x, sent, came, back, home, z, o, total, y, ring_g, ring_u, ring_d,
    ring_sem, x_sem, go_send, go_recv, back_send, back_recv,
):
    tokens, d = x.shape
    half = d // 2
    ff = sg.shape[1]
    tile = ring_g.shape[2]
    ring = ring_g.shape[0]
    per = ff // tile
    first = per * FIRST // 16
    stretches = (
        (0, first, sg, su, sd, 0),
        (first, per, wg.at[0], wu.at[0], wd.at[0], 0),
        (first + per, per, wg.at[1], wu.at[1], wd.at[1], 0),
        (first + 2 * per, per - first, sg, su, sd, first),
    )
    steps = 3 * per

    def copies(g, u, dn, tile_index, at):
        cols = pl.ds(pl.multiple_of(tile_index * tile, tile), tile)
        return (
            pltpu.make_async_copy(g.at[:, cols], ring_g.at[at], ring_sem.at[0, at]),
            pltpu.make_async_copy(u.at[:, cols], ring_u.at[at], ring_sem.at[1, at]),
            pltpu.make_async_copy(dn.at[cols, :], ring_d.at[at], ring_sem.at[2, at]),
        )

    def fetch(step):
        at = lax.rem(step, ring)
        for lo, n, g, u, dn, skip in stretches:

            @pl.when((step >= lo) & (step < lo + n))
            def _():
                for c in copies(g, u, dn, step - lo + skip, at):
                    c.start()

    def landed(step):
        at = lax.rem(step, ring)
        for c in copies(sg, su, sd, 0, at):
            c.wait()
        return at

    load_x = pltpu.make_async_copy(x_hbm, x, x_sem)
    load_x.start()
    for step in range(ring - 1):
        for c in copies(sg, su, sd, step, step):
            c.start()
    me = lax.axis_index("ep")
    my, mz, mc = me // 8, (me // 2) % 4, me % 2
    partners = [((my + a) % 2) * 8 + ((mz + b) % 4) * 2 + (mc + c) % 2 for a, b, c in OFFSETS]
    barrier = pltpu.get_barrier_semaphore()
    for p in partners:
        pl.semaphore_signal(barrier, inc=1, device_id={"ep": p}, device_id_type=MESH)

    expert, slot = expert_ref[...], slot_ref[...]
    device = lax.shift_right_logical(expert, 1)
    which = lax.bitwise_and(expert, 1)
    head = slot < HEAD
    kept = slot < SLOTS
    head_row = jnp.where(head, device * HEAD + slot, -1)
    tail_row = jnp.where(kept & ~head, device * (2 * TAIL) + slot - HEAD, -1)
    row = jnp.where(head, head_row, jnp.where(kept, N * HEAD + device * TAIL + slot - HEAD, -1))

    def one_hot(target, e, n):
        at = lax.broadcasted_iota(I32, (n, tokens), 0)
        return (at == jnp.where(which == e, target, -1)).astype(F32).astype(BF16)

    load_x.wait()
    for e in range(2):
        heads = dot(one_hot(head_row, e, N * HEAD), x[...]).astype(BF16)
        for s in range(N):
            sent[e, s, 0:HEAD] = heads[HEAD * s : HEAD * (s + 1), 0:half]
            sent[e, s, HEAD : 2 * HEAD] = heads[HEAD * s : HEAD * (s + 1), half:]
        left = dot(one_hot(tail_row, e, N * 2 * TAIL), x[:, 0:half])
        right = dot(one_hot(jnp.where(tail_row >= 0, tail_row + TAIL, -1), e, N * 2 * TAIL), x[:, half:])
        tails = (left + right).astype(BF16)
        for s in range(N):
            sent[e, s, 2 * HEAD :] = tails[2 * TAIL * s : 2 * TAIL * (s + 1)]
        came[e, me] = sent[e, me]

    pl.semaphore_wait(barrier, len(OFFSETS))

    def remote(src, dst, e, p, send, recv):
        return pltpu.make_async_remote_copy(
            src_ref=src.at[e, p], dst_ref=dst.at[e, me], send_sem=send.at[e, p], recv_sem=recv.at[e, me],
            device_id={"ep": p}, device_id_type=MESH,
        )

    def arrived(src, dst, e, p, send, recv):
        return pltpu.make_async_remote_copy(
            src_ref=src.at[e, p], dst_ref=dst.at[e, p], send_sem=send.at[e, p], recv_sem=recv.at[e, p],
            device_id={"ep": p}, device_id_type=MESH,
        )

    for e in range(2):
        for p in partners:
            remote(sent, came, e, p, go_send, go_recv).start()

    gate = gate_ref[...].astype(BF16).astype(F32)

    def stretch(which_one, lhs, acc):
        lo, n = stretches[which_one][:2]
        acc[...] = jnp.zeros_like(acc)

        @pl.loop(0, n)
        def _(j):
            step = lo + j
            fetch(step + ring - 1)
            at = landed(step)
            a = dot(lhs[...], ring_g[at])
            b = dot(lhs[...], ring_u[at])
            h = (jax.nn.silu(a) * b).astype(BF16)
            acc[...] += dot(h, ring_d[at])

    stretch(0, x, y)
    for e in range(2):
        for p in partners:
            arrived(sent, came, e, p, go_send, go_recv).wait()
        store_rows(came.at[e], z, half)
        stretch(1 + e, z, total)
        store_blocks(total, back.at[e], half)
        home[e, me] = back[e, me]
        for p in partners:
            remote(back, home, e, p, back_send, back_recv).start()

    lo, n = stretches[3][:2]

    @pl.loop(0, n)
    def _(j):
        step = lo + j
        fetch(step + ring - 1)
        at = landed(step)
        a = dot(x[...], ring_g[at])
        b = dot(x[...], ring_u[at])
        h = (jax.nn.silu(a) * b).astype(BF16)
        y[...] += dot(h, ring_d[at])

    for e in range(2):
        at = lax.broadcasted_iota(I32, (ROWS, tokens), 0)
        pick = jnp.where(at == jnp.where(which == e, row, -1), gate, 0.0).astype(BF16)
        for p in partners:
            arrived(back, home, e, p, back_send, back_recv).wait()
        store_rows(home.at[e], o, half)
        y[...] += lax.dot_general(pick, o[...], (((0,), (0,)), ((), ())), preferred_element_type=F32)
    y_ref[...] = y[...].astype(BF16)


def layer(x, expert, slot, gate, w_gate, w_up, w_down, s_gate, s_up, s_down):
    tokens, d = x.shape[2:]
    ff = s_gate.shape[1]
    tile = min(TILE, ff // 16)
    here, there = pl.BlockSpec(memory_space=pltpu.VMEM), pl.BlockSpec(memory_space=pl.ANY)
    block = (2, N, 2 * SLOTS, d // 2)
    out = pl.pallas_call(
        kernel,
        out_shape=jax.ShapeDtypeStruct((tokens, d), BF16),
        in_specs=[there, here, here, here] + [there] * 6,
        out_specs=here,
        scratch_shapes=[
            pltpu.VMEM((tokens, d), BF16),
            pltpu.VMEM(block, BF16),
            pltpu.VMEM(block, BF16),
            pltpu.VMEM(block, BF16),
            pltpu.VMEM(block, BF16),
            pltpu.VMEM((ROWS, d), BF16),
            pltpu.VMEM((ROWS, d), BF16),
            pltpu.VMEM((ROWS, d), F32),
            pltpu.VMEM((tokens, d), F32),
            pltpu.VMEM((RING, d, tile), BF16),
            pltpu.VMEM((RING, d, tile), BF16),
            pltpu.VMEM((RING, tile, d), BF16),
            pltpu.SemaphoreType.DMA((3, RING)),
            pltpu.SemaphoreType.DMA,
            pltpu.SemaphoreType.DMA((2, N)),
            pltpu.SemaphoreType.DMA((2, N)),
            pltpu.SemaphoreType.DMA((2, N)),
            pltpu.SemaphoreType.DMA((2, N)),
        ],
        compiler_params=pltpu.CompilerParams(
            collective_id=0, has_side_effects=True, vmem_limit_bytes=60 * 1024 * 1024
        ),
        name="moe",
    )(
        x.reshape(tokens, d), expert.reshape(1, tokens), slot.reshape(1, tokens), gate.reshape(1, tokens),
        w_gate, w_up, w_down, s_gate, s_up, s_down,
    )
    return out.reshape(x.shape)


def solution(mesh):
    token = P("dp", "ep", None, None)
    weight, shared = P("ep", None, None), P(None, None)
    return jax.shard_map(
        layer,
        mesh=mesh,
        in_specs=(token,) * 4 + (weight,) * 3 + (shared,) * 3,
        out_specs=token,
        check_vma=False,
    )
```

time: 226 us -> 116 us (0.51)
  matrix products: 139 us -> 0 us
  Pallas kernels: 0 us -> 113 us
  blocking collectives: 43.8 us -> 0 us
  waiting for transfers between devices: 19.3 us -> 0 us
  local copies, waits for them, and re-layouts: 14.9 us -> 2.46 us
  starting transfers between devices: 6.03 us -> 0 us
    dot_general x7 -> x0, matrix products: 139 us -> none  [einsum(): return jnp.einsum(form, a.astype(jnp.float32), b.astype(jnp.float32))]
    pallas_call x0 -> x1, Pallas kernels: none -> 113 us  [layer(): pl.pallas_call(kernel, out_shape=jax.ShapeDtypeStruct((tokens, d), BF16),...]
    another operation x1 -> x0, blocking collectives: 43.8 us -> none  [placed(): return lax.with_sharding_constraint(v, NamedSharding(mesh, P(*spec)))]
    another operation x1 -> x0, waiting for transfers between devices: 19.3 us -> none  [placed(): return lax.with_sharding_constraint(v, NamedSharding(mesh, P(*spec)))]
    another operation x4 -> x0, local copies, waits for them, and re-layouts: 10.5 us -> none  [placed(): return lax.with_sharding_constraint(v, NamedSharding(mesh, P(*spec)))]
    another operation x1 -> x0, starting transfers between devices: 6.03 us -> none  [placed(): return lax.with_sharding_constraint(v, NamedSharding(mesh, P(*spec)))]
  transfers between devices with their start and end apart: 1 -> 0, of which waited for: 1 -> 0; matrix products, arithmetic and copies ran while one was open for 8% -> 0% of each run, Pallas kernels for 0% -> 0%
where the time goes in v1:
time: 116 us
  Pallas kernels  113 us (97%)
  local copies, waits for them, and re-layouts  2.46 us (2%)
    pallas_call x1, Pallas kernels, layer(): pl.pallas_call(kernel, out_shape=jax.ShapeDtypeStruct((tokens, d), BF16),...  113 us
    unnamed x1, local copies, waits for them, and re-layouts  2.46 us

profile of v1, /device:TPU:14, one launch (start us, length us, event | category | flops | bytes accessed | tf_op | source)
XLA Modules:
  0.0 115.5 jit_solution(8429459018136551189)
XLA Ops:
  0.0 113.0 %moe.1 = bf16[512,1280]{1,0:T(8,128)(2,1)} custom-call(bf16[512,1280]{1,0:T(8,128)(2,1)} %bitcast.6, s32[1,512]{1,0:T(1,128)} %bitcast.7, s32[1,512]{1,0:T(1,128)} %bitcast.8, f32[1,512]{1,0:T(1,128)} %bitcast.9, bf16[2,1280,8192]{2,1,0:T(8,128)(2,1)} %wg.1, bf16[2,1280,8192]{2,1,0:T(8,128)(2,1)} %wu.1, bf16[2,8192,1280]{2,1,0:T(8,128)(2,1)} %wd.1, ...), custom_call_target="tpu_custom_call" | custom-call | tf_op jit(solution)/shard_map/moe/pallas_call | solution.py:218
  113.1 2.5 %copy.12 = bf16[1,1,512,1280]{3,2,1,0:T(8,128)(2,1)} copy(bf16[1,1,512,1280]{3,2,1,0:T(8,128)(2,1)} %bitcast.5) | data formatting | bytes 2621440

commit v2 on v1

--- a/solution.py
+++ b/solution.py
@@ -12,9 +12,11 @@
 SLOTS, HEAD = 20, 16
 TAIL = SLOTS - HEAD
 ROWS = N * SLOTS
-TILE = 512
+TILE = 1024
 RING = 5
 FIRST = 8
+PAIR = 2
+LIMIT = 63 * 1024 * 1024
 
 BF16, F32, I32 = jnp.bfloat16, jnp.float32, jnp.int32
 OFFSETS = [(y, z, c) for z in (2, 1, 3, 0) for y in (1, 0) for c in (1, 0) if (y, z, c) != (0, 0, 0)]
@@ -63,7 +65,7 @@
 
 def kernel(
     x_hbm, expert_ref, slot_ref, gate_ref, wg, wu, wd, sg, su, sd, y_ref,
-    x, sent, came, back, home, z, o, total, y, ring_g, ring_u, ring_d,
+    x, hid, sent, came, home, z, total, y, ring_g, ring_u, ring_d,
     ring_sem, x_sem, go_send, go_recv, back_send, back_recv,
 ):
     tokens, d = x.shape
@@ -106,9 +108,6 @@
 
     load_x = pltpu.make_async_copy(x_hbm, x, x_sem)
     load_x.start()
-    for step in range(ring - 1):
-        for c in copies(sg, su, sd, step, step):
-            c.start()
     me = lax.axis_index("ep")
     my, mz, mc = me // 8, (me // 2) % 4, me % 2
     partners = [((my + a) % 2) * 8 + ((mz + b) % 4) * 2 + (mc + c) % 2 for a, b, c in OFFSETS]
@@ -129,8 +128,7 @@
         at = lax.broadcasted_iota(I32, (n, tokens), 0)
         return (at == jnp.where(which == e, target, -1)).astype(F32).astype(BF16)
 
-    load_x.wait()
-    for e in range(2):
+    def pack(e):
         heads = dot(one_hot(head_row, e, N * HEAD), x[...]).astype(BF16)
         for s in range(N):
             sent[e, s, 0:HEAD] = heads[HEAD * s : HEAD * (s + 1), 0:half]
@@ -142,8 +140,6 @@
             sent[e, s, 2 * HEAD :] = tails[2 * TAIL * s : 2 * TAIL * (s + 1)]
         came[e, me] = sent[e, me]
 
-    pl.semaphore_wait(barrier, len(OFFSETS))
-
     def remote(src, dst, e, p, send, recv):
         return pltpu.make_async_remote_copy(
             src_ref=src.at[e, p], dst_ref=dst.at[e, me], send_sem=send.at[e, p], recv_sem=recv.at[e, me],
@@ -156,63 +152,69 @@
             device_id={"ep": p}, device_id_type=MESH,
         )
 
-    for e in range(2):
+    load_x.wait()
+    for step in range(ring - PAIR):
+        for c in copies(sg, su, sd, step, step):
+            c.start()
+    pack(0)
+    pl.semaphore_wait(barrier, len(OFFSETS))
+    for p in partners:
+        remote(sent, came, 0, p, go_send, go_recv).start()
+    pack(1)
+
+    gate = gate_ref[...].astype(BF16).astype(F32)
+
+    def stretch(which_one, lhs, acc, fresh=True):
+        lo, n = stretches[which_one][:2]
+        m = lhs.shape[0]
+        if fresh:
+            acc[...] = jnp.zeros_like(acc)
+
+        @pl.loop(0, n // PAIR)
+        def _(j):
+            step = lo + j * PAIR
+            for i in range(PAIR):
+                fetch(step + ring - PAIR + i)
+            at = [landed(step + i) for i in range(PAIR)]
+            for i in range(PAIR):
+                a = dot(lhs[...], ring_g[at[i]])
+                b = dot(lhs[...], ring_u[at[i]])
+                hid[i, 0:m] = (jax.nn.silu(a) * b).astype(BF16)
+            for i in range(PAIR):
+                acc[...] += dot(hid[i, 0:m], ring_d[at[i]])
+
+    def wait_go(e):
         for p in partners:
-            remote(sent, came, e, p, go_send, go_recv).start()
-
-    gate = gate_ref[...].astype(BF16).astype(F32)
-
-    def stretch(which_one, lhs, acc):
-        lo, n = stretches[which_one][:2]
-        acc[...] = jnp.zeros_like(acc)
-
-        @pl.loop(0, n)
-        def _(j):
-            step = lo + j
-            fetch(step + ring - 1)
-            at = landed(step)
-            a = dot(lhs[...], ring_g[at])
-            b = dot(lhs[...], ring_u[at])
-            h = (jax.nn.silu(a) * b).astype(BF16)
-            acc[...] += dot(h, ring_d[at])
+            arrived(sent, came, e, p, go_send, go_recv).wait()
 
     stretch(0, x, y)
     for e in range(2):
-        for p in partners:
-            arrived(sent, came, e, p, go_send, go_recv).wait()
+        wait_go(e)
+        if e == 0:
+            for p in partners:
+                remote(sent, came, 1, p, go_send, go_recv).start()
         store_rows(came.at[e], z, half)
         stretch(1 + e, z, total)
-        store_blocks(total, back.at[e], half)
-        home[e, me] = back[e, me]
+        store_blocks(total, sent.at[e], half)
+        home[e, me] = sent[e, me]
         for p in partners:
-            remote(back, home, e, p, back_send, back_recv).start()
-
-    lo, n = stretches[3][:2]
-
-    @pl.loop(0, n)
-    def _(j):
-        step = lo + j
-        fetch(step + ring - 1)
-        at = landed(step)
-        a = dot(x[...], ring_g[at])
-        b = dot(x[...], ring_u[at])
-        h = (jax.nn.silu(a) * b).astype(BF16)
-        y[...] += dot(h, ring_d[at])
+            remote(sent, home, e, p, back_send, back_recv).start()
+    stretch(3, x, y, False)
 
     for e in range(2):
         at = lax.broadcasted_iota(I32, (ROWS, tokens), 0)
         pick = jnp.where(at == jnp.where(which == e, row, -1), gate, 0.0).astype(BF16)
         for p in partners:
-            arrived(back, home, e, p, back_send, back_recv).wait()
-        store_rows(home.at[e], o, half)
-        y[...] += lax.dot_general(pick, o[...], (((0,), (0,)), ((), ())), preferred_element_type=F32)
+            arrived(sent, home, e, p, back_send, back_recv).wait()
+        store_rows(home.at[e], z, half)
+        y[...] += lax.dot_general(pick, z[...], (((0,), (0,)), ((), ())), preferred_element_type=F32)
     y_ref[...] = y[...].astype(BF16)
 
 
 def layer(x, expert, slot, gate, w_gate, w_up, w_down, s_gate, s_up, s_down):
     tokens, d = x.shape[2:]
     ff = s_gate.shape[1]
-    tile = min(TILE, ff // 16)
+    tile = min(TILE, ff // 8)
     here, there = pl.BlockSpec(memory_space=pltpu.VMEM), pl.BlockSpec(memory_space=pl.ANY)
     block = (2, N, 2 * SLOTS, d // 2)
     out = pl.pallas_call(
@@ -222,11 +224,10 @@
         out_specs=here,
         scratch_shapes=[
             pltpu.VMEM((tokens, d), BF16),
+            pltpu.VMEM((PAIR, tokens, tile), BF16),
             pltpu.VMEM(block, BF16),
             pltpu.VMEM(block, BF16),
             pltpu.VMEM(block, BF16),
-            pltpu.VMEM(block, BF16),
-            pltpu.VMEM((ROWS, d), BF16),
             pltpu.VMEM((ROWS, d), BF16),
             pltpu.VMEM((ROWS, d), F32),
             pltpu.VMEM((tokens, d), F32),
@@ -241,7 +242,7 @@
             pltpu.SemaphoreType.DMA((2, N)),
         ],
         compiler_params=pltpu.CompilerParams(
-            collective_id=0, has_side_effects=True, vmem_limit_bytes=60 * 1024 * 1024
+            collective_id=0, has_side_effects=True, vmem_limit_bytes=LIMIT
         ),
         name="moe",
     )(

time: 116 us -> 94.3 us (0.81)
  Pallas kernels: 113 us -> 91.6 us
    pallas_call x1, Pallas kernels: 113 us -> 91.6 us  [layer(): pl.pallas_call(kernel, out_shape=jax.ShapeDtypeStruct((tokens, d), BF16),...]
where the time goes in v2:
time: 94.3 us; the launch traced here: 94.1 us
  Pallas kernels  91.6 us (97%)
  local copies, waits for them, and re-layouts  2.46 us (3%)
    pallas_call x1, Pallas kernels, layer(): pl.pallas_call(kernel, out_shape=jax.ShapeDtypeStruct((tokens, d), BF16),...  91.6 us
    unnamed x1, local copies, waits for them, and re-layouts  2.46 us

profile of v2, /device:TPU:14, one launch (start us, length us, event | category | flops | bytes accessed | tf_op | source)
XLA Modules:
  0.0 94.1 jit_solution(6835067497149463595)
XLA Ops:
  0.0 91.6 %moe.1 = bf16[512,1280]{1,0:T(8,128)(2,1)} custom-call(bf16[512,1280]{1,0:T(8,128)(2,1)} %bitcast.6, s32[1,512]{1,0:T(1,128)} %bitcast.7, s32[1,512]{1,0:T(1,128)} %bitcast.8, f32[1,512]{1,0:T(1,128)} %bitcast.9, bf16[2,1280,8192]{2,1,0:T(8,128)(2,1)} %wg.1, bf16[2,1280,8192]{2,1,0:T(8,128)(2,1)} %wu.1, bf16[2,8192,1280]{2,1,0:T(8,128)(2,1)} %wd.1, ...), custom_call_target="tpu_custom_call" | custom-call | tf_op jit(solution)/shard_map/moe/pallas_call | solution.py:220
  91.6 2.5 %copy.12 = bf16[1,1,512,1280]{3,2,1,0:T(8,128)(2,1)} copy(bf16[1,1,512,1280]{3,2,1,0:T(8,128)(2,1)} %bitcast.5) | data formatting | bytes 2621440

commit v3 on v2

--- a/solution.py
+++ b/solution.py
@@ -15,6 +15,7 @@
 TILE = 1024
 RING = 5
 FIRST = 8
+ONE = 1
 PAIR = 2
 LIMIT = 63 * 1024 * 1024
 
@@ -153,53 +154,58 @@
         )
 
     load_x.wait()
-    for step in range(ring - PAIR):
+    def begin(step):
         for c in copies(sg, su, sd, step, step):
             c.start()
+
+    begin(0)
     pack(0)
     pl.semaphore_wait(barrier, len(OFFSETS))
     for p in partners:
         remote(sent, came, 0, p, go_send, go_recv).start()
+    begin(1)
     pack(1)
+    for step in range(2, ring - PAIR):
+        begin(step)
 
     gate = gate_ref[...].astype(BF16).astype(F32)
 
-    def stretch(which_one, lhs, acc, fresh=True):
+    def stretch(which_one, lhs, acc, count):
         lo, n = stretches[which_one][:2]
         m = lhs.shape[0]
-        if fresh:
-            acc[...] = jnp.zeros_like(acc)
-
-        @pl.loop(0, n // PAIR)
+
+        @pl.loop(0, n // count)
         def _(j):
-            step = lo + j * PAIR
-            for i in range(PAIR):
+            step = lo + j * count
+            for i in range(count):
                 fetch(step + ring - PAIR + i)
-            at = [landed(step + i) for i in range(PAIR)]
-            for i in range(PAIR):
+            at = [landed(step + i) for i in range(count)]
+            for i in range(count):
                 a = dot(lhs[...], ring_g[at[i]])
                 b = dot(lhs[...], ring_u[at[i]])
                 hid[i, 0:m] = (jax.nn.silu(a) * b).astype(BF16)
-            for i in range(PAIR):
+            for i in range(count):
                 acc[...] += dot(hid[i, 0:m], ring_d[at[i]])
 
     def wait_go(e):
         for p in partners:
             arrived(sent, came, e, p, go_send, go_recv).wait()
 
-    stretch(0, x, y)
+    y[...] = jnp.zeros_like(y)
+    stretch(0, x, y, ONE)
     for e in range(2):
         wait_go(e)
         if e == 0:
             for p in partners:
                 remote(sent, came, 1, p, go_send, go_recv).start()
         store_rows(came.at[e], z, half)
-        stretch(1 + e, z, total)
+        total[...] = jnp.zeros_like(total)
+        stretch(1 + e, z, total, PAIR)
         store_blocks(total, sent.at[e], half)
         home[e, me] = sent[e, me]
         for p in partners:
             remote(sent, home, e, p, back_send, back_recv).start()
-    stretch(3, x, y, False)
+    stretch(3, x, y, PAIR)
 
     for e in range(2):
         at = lax.broadcasted_iota(I32, (ROWS, tokens), 0)

time: 94.3 us -> 93.3 us (0.989)
  Pallas kernels: 91.6 us -> 90.2 us
    pallas_call x1, Pallas kernels: 91.6 us -> 90.2 us  [layer(): pl.pallas_call(kernel, out_shape=jax.ShapeDtypeStruct((tokens, d), BF16),...]
where the time goes in v3:
time: 93.3 us; the launch traced here: 92.7 us
  Pallas kernels  90.2 us (97%)
  local copies, waits for them, and re-layouts  2.46 us (3%)
    pallas_call x1, Pallas kernels, layer(): pl.pallas_call(kernel, out_shape=jax.ShapeDtypeStruct((tokens, d), BF16),...  90.2 us
    unnamed x1, local copies, waits for them, and re-layouts  2.46 us

profile of v3, /device:TPU:14, one launch (start us, length us, event | category | flops | bytes accessed | tf_op | source)
XLA Modules:
  0.0 92.7 jit_solution(385611939719854470)
XLA Ops:
  0.0 90.2 %moe.1 = bf16[512,1280]{1,0:T(8,128)(2,1)} custom-call(bf16[512,1280]{1,0:T(8,128)(2,1)} %bitcast.6, s32[1,512]{1,0:T(1,128)} %bitcast.7, s32[1,512]{1,0:T(1,128)} %bitcast.8, f32[1,512]{1,0:T(1,128)} %bitcast.9, bf16[2,1280,8192]{2,1,0:T(8,128)(2,1)} %wg.1, bf16[2,1280,8192]{2,1,0:T(8,128)(2,1)} %wu.1, bf16[2,8192,1280]{2,1,0:T(8,128)(2,1)} %wd.1, ...), custom_call_target="tpu_custom_call" | custom-call | tf_op jit(solution)/shard_map/moe/pallas_call | solution.py:226
  90.2 2.5 %copy.12 = bf16[1,1,512,1280]{3,2,1,0:T(8,128)(2,1)} copy(bf16[1,1,512,1280]{3,2,1,0:T(8,128)(2,1)} %bitcast.5) | data formatting | bytes 2621440
